TPU v7x, 32 devices: a whole 2x2x4 slice. The times are simulated.
32 devices in a mesh: dp: 4 (over y, core), ctx: 8 (over z, x).
Axes of the slice: x: 2, y: 2, z: 4, core: 2. Of those that a mesh axis runs over, the one named last changes fastest.
Arguments:
- text: bfloat16 [4, 2, 128, 2048], P('dp', None, None, 'ctx'), may hold values from -6 to 6
- src: int32 [4], replicated, may hold values from 0 to 3, each once
- lengths: int32 [4, 2], replicated, may hold values from 1 to 128
- kv_weight: bfloat16 [2048, 2, 8192], P('dp', None, 'ctx'), may hold values from -0.125 to 0.125
- queries: bfloat16 [4, 2048, 4096], P('dp', 'ctx'), may hold values from -160 to 160
- grad_out: bfloat16 [4, 2048, 4096], P('dp', 'ctx'), may hold values from -6 to 6
Outputs:
- attended: bfloat16 [4, 2048, 4096], P('dp', 'ctx')
- grad_queries: bfloat16 [4, 2048, 4096], P('dp', 'ctx')
- grad_weight: float32 [2048, 2, 8192], P('dp', None, 'ctx')
Inputs may be any that keep to these rules, and one draw needn't show every extreme that they name: `src`: each text sample is used by exactly one latent sample. `lengths`: tokens of an encoder output at or beyond its length are padding.
All inputs are finite; a program needn't handle non-finite values.
Results may differ from a plain program's by a relative error of at most 0.018.
The roundings to bfloat16 on the way count: a program that leaves them out, or rounds other values in their place, can miss the bound.
Values may be sent and summed in bfloat16 or wider, within the bound.
A program may use at most 128 MiB of HBM per device.

v0:
```python
import math
import jax
import jax.numpy as jnp
from jax import lax
from jax.sharding import PartitionSpec as P

HEAD = 128


def attend(queries, key_value, valid, grad_out):
    batch, length, width = queries.shape
    heads = width // HEAD
    keys = key_value.shape[1] * key_value.shape[2]
    scale = 1.0 / math.sqrt(HEAD)
    paired = key_value.reshape(batch, keys, heads, 2, HEAD)
    key = paired[:, :, :, 0]
    value = paired[:, :, :, 1]
    q_rows = queries.reshape(batch, length, heads, HEAD)
    g_rows = grad_out.reshape(batch, length, heads, HEAD)
    scores = jnp.einsum("blhd,bjhd->bhlj", q_rows, key, preferred_element_type=jnp.float32) * scale
    scores = jnp.where(valid[:, None, None, :], scores, -1e30)
    top = jnp.max(scores, axis=-1, keepdims=True)
    weights = jnp.exp(scores - top)
    probs = weights / jnp.sum(weights, axis=-1, keepdims=True)
    probs_low = probs.astype(jnp.bfloat16)
    attended = jnp.einsum("bhlj,bjhd->blhd", probs_low, value, preferred_element_type=jnp.float32)
    attended = attended.reshape(batch, length, width).astype(jnp.bfloat16)
    grad_probs = jnp.einsum("blhd,bjhd->bhlj", g_rows, value, preferred_element_type=jnp.float32)
    delta = jnp.sum(probs * grad_probs, axis=-1, keepdims=True)
    grad_scores = (probs * (grad_probs - delta) * scale).astype(jnp.bfloat16)
    grad_queries = jnp.einsum(
        "bhlj,bjhd->blhd", grad_scores, key, preferred_element_type=jnp.float32
    )
    grad_queries = grad_queries.reshape(batch, length, width).astype(jnp.bfloat16)
    grad_key = jnp.einsum(
        "bhlj,blhd->bjhd", grad_scores, q_rows, preferred_element_type=jnp.float32
    )
    grad_value = jnp.einsum(
        "bhlj,blhd->bjhd", probs_low, g_rows, preferred_element_type=jnp.float32
    )
    grad_kv = jnp.stack([grad_key, grad_value], axis=3).reshape(
        batch, 2, keys // 2, heads * 2 * HEAD
    )
    return (attended, grad_queries, grad_kv)


def per_device(text, src, lengths, kv_weight, queries, grad_out):
    per_group = queries.shape[0]
    group = lax.axis_index("dp")
    everyone = lax.all_gather(text, "dp", axis=0, tiled=True)
    chosen_ids = lax.dynamic_slice_in_dim(src, group * per_group, per_group, 0)
    picked = jnp.take(everyone, chosen_ids, axis=0)
    full_text = lax.all_gather(picked, "ctx", axis=3, tiled=True)
    tokens = full_text.shape[2]
    rows = full_text
    kv_local = jnp.einsum(
        "betf,fec->betc",
        rows,
        lax.all_gather(kv_weight, "dp", axis=0, tiled=True),
        preferred_element_type=jnp.float32,
    ).astype(jnp.bfloat16)
    chosen_lengths = jnp.take(lengths, chosen_ids, axis=0)
    positions = jnp.arange(tokens, dtype=jnp.int32)
    valid = (positions[None, None, :] < chosen_lengths[:, :, None]).reshape(per_group, 2 * tokens)
    moved_queries, moved_grads = (
        lax.all_to_all(queries, "ctx", split_axis=2, concat_axis=1, tiled=True),
        lax.all_to_all(grad_out, "ctx", split_axis=2, concat_axis=1, tiled=True),
    )
    head_out, head_grad, grad_kv = attend(moved_queries, kv_local, valid, moved_grads)
    attended, grad_queries = (
        lax.all_to_all(head_out, "ctx", split_axis=1, concat_axis=2, tiled=True),
        lax.all_to_all(head_grad, "ctx", split_axis=1, concat_axis=2, tiled=True),
    )
    grad_low = grad_kv.astype(jnp.bfloat16)
    rows = full_text
    grad_weight = lax.psum_scatter(
        jnp.einsum("betf,betc->fec", rows, grad_low, preferred_element_type=jnp.float32).astype(
            jnp.bfloat16
        ),
        "dp",
        scatter_dimension=0,
        tiled=True,
    ).astype(jnp.float32)
    return (attended, grad_queries, grad_weight)


def solution(mesh):
    placed = (
        P("dp", None, None, "ctx"),
        P(),
        P(),
        P("dp", None, "ctx"),
        P("dp", "ctx", None),
        P("dp", "ctx", None),
    )
    return jax.shard_map(
        per_device,
        mesh=mesh,
        in_specs=placed,
        out_specs=(P("dp", "ctx", None), P("dp", "ctx", None), P("dp", None, "ctx")),
        check_vma=False,
    )
```

profile of v0, /device:TPU:0, one launch (start us, length us, event | category | flops | bytes accessed | tf_op | source)
XLA Modules:
  0.0 400.6 jit_solution(18149222278047048982)
XLA Ops:
  7.2 0.0 all-gather.3.cloned.1.call-start
  7.2 1.4 dynamic_slice.3
  10.6 8.9 %all_gather.9 = bf16[4,2,128,256]{3,2,1,0:T(8,128)(2,1)S(1)} all-gather(bf16[1,2,128,256]{3,2,1,0:T(8,128)(2,1)} %param.6), channel_id=1, replica_groups=mesh['dp'=4,'ctx'=8] {'dp'}, dimensions={0}, use_global_device_ids=true | all-gather | bytes 655360 | tf_op jit(solution)/shard_map/all_gather | solution.py:50
  19.4 0.7 dynamic-slice_select_fusion
  20.1 0.0 all-gather.3.cloned.1.call-update
  20.1 0.0 all-gather.5.cloned.1.call-start
  20.2 3.5 copy.79
  23.7 7.1 %copy.82 = bf16[1,256,4096]{1,0,2:T(2,128)(2,1)} copy(bf16[1,256,4096]{2,1,0:T(8,128)(2,1)S(1)} %copy-done.1) | data formatting | bytes 4194304 | tf_op args[4]
  30.8 0.5 broadcast.122
  31.3 21.5 %reduce.8 = bf16[4096,256]{1,0:T(8,128)(2,1)S(1)} reduce(bf16[4096,1,256]{2,1,0:T(2,128)(2,1)} %bitcast.142, bf16[]{:T(256)} %broadcast.122), dimensions={1}, to_apply=%bitcast.123.reduce_sub_computation | reduce | bytes 4194306
  52.8 3.2 reshape.226
  56.0 5.8 %all-to-all-start = ((bf16[8,2,65536]{2,1,0:T(2,128)(2,1)}), bf16[8,2,65536]{2,1,0:T(2,128)(2,1)S(1)}, u32[]{:S(2)}, u32[]{:S(2)}) async-start(bf16[8,2,65536]{2,1,0:T(2,128)(2,1)} %reshape.226), calls=%async_computation | async-start | bytes 4194304 | tf_op jit(solution)/shard_map/all_to_all | solution.py:66
  61.8 10.1 %copy.88 = bf16[1,256,4096]{1,0,2:T(2,128)(2,1)} copy(bf16[1,256,4096]{2,1,0:T(8,128)(2,1)} %param.11) | data formatting | bytes 4194304 | tf_op args[5]
  71.9 22.8 %reduce.10 = bf16[4096,256]{1,0:T(8,128)(2,1)} reduce(bf16[4096,1,256]{2,1,0:T(2,128)(2,1)} %bitcast.149, bf16[]{:T(256)} %broadcast.122), dimensions={1}, to_apply=%bitcast.121.reduce_sub_computation | reduce | bytes 4194306
  94.7 5.8 %reshape.224 = bf16[8,2,65536]{2,1,0:T(2,128)(2,1)} reshape(bf16[4096,256]{1,0:T(8,128)(2,1)} %reduce.10) | data formatting | bytes 4194304
  100.6 10.0 %all-to-all-done = bf16[8,2,65536]{2,1,0:T(2,128)(2,1)S(1)} async-done(((bf16[8,2,65536]{2,1,0:T(2,128)(2,1)}), bf16[8,2,65536]{2,1,0:T(2,128)(2,1)S(1)}, u32[]{:S(2)}, u32[]{:S(2)}) %all-to-all-start) | async-done | bytes 2097184 | tf_op jit(solution)/shard_map/all_to_all | solution.py:66
  110.5 4.4 %all-to-all-start.2 = ((bf16[8,2,65536]{2,1,0:T(2,128)(2,1)}), bf16[8,2,65536]{2,1,0:T(2,128)(2,1)}, u32[]{:S(2)}, u32[]{:S(2)}) async-start(bf16[8,2,65536]{2,1,0:T(2,128)(2,1)} %reshape.224), calls=%async_computation.2 | async-start | bytes 4194304 | tf_op jit(solution)/shard_map/all_to_all | solution.py:67
  114.9 0.3 reduce-scatter.2.cloned.1.call-start
  115.3 0.2 fusion.35
  115.4 0.1 lt.36
  115.5 4.3 %reshape.227 = bf16[4096,1,256]{2,1,0:T(2,128)(2,1)} reshape(bf16[8,2,65536]{2,1,0:T(2,128)(2,1)S(1)} %all-to-all-done) | data formatting | bytes 4194304
  119.8 2.5 copy.112
  122.4 1.2 copy.83
  123.6 2.3 reshape.172
  125.9 36.9 %all-to-all-done.2 = bf16[8,2,65536]{2,1,0:T(2,128)(2,1)} async-done(((bf16[8,2,65536]{2,1,0:T(2,128)(2,1)}), bf16[8,2,65536]{2,1,0:T(2,128)(2,1)}, u32[]{:S(2)}, u32[]{:S(2)}) %all-to-all-start.2) | async-done | bytes 2097184 | tf_op jit(solution)/shard_map/all_to_all | solution.py:67
  162.8 6.7 %reshape.225 = bf16[4096,1,256]{2,1,0:T(2,128)(2,1)} reshape(bf16[8,2,65536]{2,1,0:T(2,128)(2,1)} %all-to-all-done.2) | data formatting | bytes 4194304
  169.5 2.5 copy.114
  172.1 2.5 copy.89
  174.6 2.9 reshape.173
  177.5 0.0 all-gather.3.cloned.1.call-done
  177.5 0.0 all-gather.5.cloned.1.call-done
  177.5 5.0 %fusion.19 = bf16[1,2,128,1024]{3,2,1,0:T(8,128)(2,1)S(1)} fusion(bf16[2048,2,1024]{2,0,1:T(8,128)(2,1)} %all-gather.5.cloned.1.call-done, bf16[1,2,128,2048]{3,2,1,0:T(8,128)(2,1)} %all-gather.3.cloned.1.call-done), kind=kOutput, calls=%fused_computation.26 | convolution fusion | flops 1074003968 | bytes 9961472 | tf_op jit(solution)/shard_map/betf,fec->betc/dot_general | solution.py:56
  182.5 0.4 reshape.169
  182.9 1.5 fusion.42
  184.4 1.0 copy.116
  185.4 4.5 %fusion.32 = f32[4,256,2048]{2,1,0:T(8,128)} fusion(bf16[2048,4,128]{0,2,1:T(8,128)(2,1)S(1)} %reshape.173, bf16[1,256,4,1,128]{1,4,2,3,0:T(8,128)(2,1)S(1)} %copy.116), kind=kOutput, calls=%fused_computation.36 | convolution fusion | flops 536870912 | bytes 10747904 | tf_op jit(solution)/shard_map/blhd,bjhd->bhlj/dot_general | solution.py:28
  189.9 8.0 %fusion.43 = (f32[4,2048]{1,0:T(4,128)S(1)}, f32[4,2048,256]{1,2,0:T(8,128)}) fusion(pred[256]{0:T(512)(128)(4,1)S(1)} %bitcast_compare_fusion, bf16[2048,4,128]{0,2,1:T(8,128)(2,1)} %reshape.172, bf16[1,256,4,1,128]{4,3,2,1,0:T(2,128)(2,1)S(1)} %copy-done.2), kind=kOutput, calls=%fused_computation.50 | convolution fusion | flops 545259776 | bytes 10780928 | tf_op jit(solution)/shard_map/sub | solution.py:23
  197.9 4.6 %fusion.24 = bf16[1,256,4,1,128]{4,1,2,3,0:T(8,128)(2,1)S(1)} fusion(bf16[2048,4,128]{0,2,1:T(8,128)(2,1)S(1)} %reshape.173, f32[4,2048,256]{1,2,0:T(8,128)} %get-tuple-element.43, f32[4,2048]{1,0:T(4,128)S(1)} %get-tuple-element.42), kind=kOutput, calls=%fused_computation.29 | convolution fusion | flops 541196288 | bytes 10780672 | tf_op jit(solution)/shard_map/bhlj,blhd->bjhd/dot_general | solution.py:38
  202.6 14.9 %fusion.27 = bf16[1,256,4,1,128]{4,1,2,3,0:T(8,128)(2,1)S(1)} fusion(bf16[2048,4,128]{0,2,1:T(8,128)(2,1)} %reshape.172, f32[4,256,2048]{2,1,0:T(8,128)} %fusion.32, f32[4,2048,256]{1,2,0:T(8,128)} %get-tuple-element.43, f32[4,2048]{1,0:T(4,128)S(1)} %get-tuple-element.42), kind=kOutput, calls=%fused_computation.30 | convolution fusion | flops 551690496 | bytes 19169280 | tf_op jit(solution)/shard_map/bhlj,blhd->bjhd/dot_general | solution.py:35
  217.4 0.1 pad_maximum_fusion
  217.5 0.5 copy.98
  218.1 0.4 convert_element_type.90
  218.4 5.6 %convert_bitcast_fusion = bf16[2048,2,1024]{0,2,1:T(8,128)(2,1)} fusion(bf16[2,128,1024]{2,1,0:T(8,128)(2,1)S(1)} %convert_element_type.90, bf16[1,2,128,2048]{3,2,1,0:T(8,128)(2,1)S(1)} %copy-done), kind=kOutput, calls=%fused_computation.11 | convolution fusion | flops 1077936128 | bytes 9961472 | tf_op jit(solution)/shard_map/betf,betc->fec/dot_general | solution.py:77
  224.0 18.2 %fusion.15 = bf16[4,128,2048]{2,1,0:T(8,128)(2,1)S(1)} fusion(f32[4,256,2048]{2,1,0:T(8,128)} %fusion.32, bf16[1,256,4,1,128]{4,3,2,1,0:T(2,128)(2,1)S(1)} %copy-done.2, f32[4,2048,256]{1,2,0:T(8,128)} %get-tuple-element.43, f32[4,2048]{1,0:T(4,128)S(1)} %get-tuple-element.42), kind=kOutput, calls=%fused_computation.20 | convolution fusion | flops 552608000 | bytes 19169280 | tf_op jit(solution)/shard_map/bhlj,bjhd->blhd/dot_general | solution.py:31
  242.3 7.5 %copy.94 = bf16[1,2048,512]{2,0,1:T(2,128)(2,1)} copy(bf16[1,2048,512]{1,2,0:T(8,128)(2,1)S(1)} %bitcast.157) | data formatting | bytes 4194304 | tf_op jit(solution)/shard_map/convert_element_type | solution.py:34
  249.8 14.0 %reduce.11 = bf16[2048,512]{1,0:T(8,128)(2,1)S(1)} reduce(bf16[2048,1,512]{2,1,0:T(2,128)(2,1)} %bitcast.146, bf16[]{:T(256)} %broadcast.122), dimensions={1}, to_apply=%bitcast.127.reduce_sub_computation | reduce | bytes 4194306
  263.8 3.8 reshape.230
  267.6 3.6 all-to-all-start.3
  271.2 5.7 %convolution_convert_fusion = bf16[4,128,2048]{2,1,0:T(8,128)(2,1)} fusion(bf16[1,256,4,1,128]{1,4,2,3,0:T(8,128)(2,1)S(1)} %copy.116, f32[4,2048,256]{1,2,0:T(8,128)} %get-tuple-element.43, f32[4,2048]{1,0:T(4,128)S(1)} %get-tuple-element.42), kind=kOutput, calls=%fused_computation.21 | convolution fusion | flops 542113792 | bytes 10780672 | tf_op jit(solution)/shard_map/bhlj,bjhd->blhd/dot_general | solution.py:26
  276.9 10.8 %copy.86 = bf16[1,2048,512]{2,0,1:T(2,128)(2,1)} copy(bf16[1,2048,512]{1,2,0:T(8,128)(2,1)} %bitcast.156) | data formatting | bytes 4194304 | tf_op jit(solution)/shard_map/convert_element_type | solution.py:27
  287.6 15.3 %reduce.9 = bf16[2048,512]{1,0:T(8,128)(2,1)} reduce(bf16[2048,1,512]{2,1,0:T(2,128)(2,1)} %bitcast.143, bf16[]{:T(256)} %broadcast.122), dimensions={1}, to_apply=%bitcast.125.reduce_sub_computation | reduce | bytes 4194306
  302.9 6.3 %reshape.228 = bf16[8,2,65536]{2,1,0:T(2,128)(2,1)} reshape(bf16[2048,512]{1,0:T(8,128)(2,1)} %reduce.9) | data formatting | bytes 4194304
  309.2 9.8 %all-to-all-done.3 = bf16[8,2,65536]{2,1,0:T(2,128)(2,1)S(1)} async-done(((bf16[8,2,65536]{2,1,0:T(2,128)(2,1)}), bf16[8,2,65536]{2,1,0:T(2,128)(2,1)S(1)}, u32[]{:S(2)}, u32[]{:S(2)}) %all-to-all-start.3) | async-done | bytes 2097184 | tf_op jit(solution)/shard_map/all_to_all | solution.py:72
  319.1 4.6 %all-to-all-start.1 = ((bf16[8,2,65536]{2,1,0:T(2,128)(2,1)}), bf16[8,2,65536]{2,1,0:T(2,128)(2,1)}, u32[]{:S(2)}, u32[]{:S(2)}) async-start(bf16[8,2,65536]{2,1,0:T(2,128)(2,1)} %reshape.228), calls=%async_computation.1 | async-start | bytes 4194304 | tf_op jit(solution)/shard_map/all_to_all | solution.py:71
  323.6 4.3 %reshape.231 = bf16[2048,1,512]{2,1,0:T(2,128)(2,1)} reshape(bf16[8,2,65536]{2,1,0:T(2,128)(2,1)S(1)} %all-to-all-done.3) | data formatting | bytes 4194304
  328.0 2.8 copy.115
  330.8 2.4 copy.95
  333.1 4.1 %copy.101 = bf16[1,256,4096]{2,1,0:T(8,128)(2,1)} copy(bf16[1,256,4096]{1,2,0:T(8,128)(2,1)} %bitcast.154) | data formatting | bytes 4194304
  337.2 34.2 %all-to-all-done.1 = bf16[8,2,65536]{2,1,0:T(2,128)(2,1)} async-done(((bf16[8,2,65536]{2,1,0:T(2,128)(2,1)}), bf16[8,2,65536]{2,1,0:T(2,128)(2,1)}, u32[]{:S(2)}, u32[]{:S(2)}) %all-to-all-start.1) | async-done | bytes 2097184 | tf_op jit(solution)/shard_map/all_to_all | solution.py:71
  371.4 6.7 %reshape.229 = bf16[2048,1,512]{2,1,0:T(2,128)(2,1)} reshape(bf16[8,2,65536]{2,1,0:T(2,128)(2,1)} %all-to-all-done.1) | data formatting | bytes 4194304
  378.2 2.8 copy.113
  381.0 2.4 copy.87
  383.3 4.1 %copy.100 = bf16[1,256,4096]{2,1,0:T(8,128)(2,1)} copy(bf16[1,256,4096]{1,2,0:T(8,128)(2,1)} %bitcast.155) | data formatting | bytes 4194304
  387.4 6.5 %copy.102 = f32[512,2,1024]{2,1,0:T(2,128)} copy(bf16[512,2,1024]{0,2,1:T(8,128)(2,1)} %reduce-scatter.2.cloned.1.call-done) | data formatting | bytes 6291456
  (12 shorter events, 0.1 us)
Async XLA Ops:
  7.2 16.6 %copy-start.1 = (bf16[1,256,4096]{2,1,0:T(8,128)(2,1)S(1)}, bf16[1,256,4096]{2,1,0:T(8,128)(2,1)}, u32[]{:S(2)}) copy-start(bf16[1,256,4096]{2,1,0:T(8,128)(2,1)} %param.10) | copy-start | bytes 6291460
  7.2 170.3 %all-gather.3.cloned.1.call-start = ((), (), s32[]{:S(2)}) async-start(), calls=%async_computation.5 | async-start | bytes 1179648 | tf_op jit(solution)/shard_map/all_gather | solution.py:53
  20.1 157.4 %all-gather.5.cloned.1.call-start = ((), (), s32[]{:S(2)}) async-start(), calls=%async_computation.6 | async-start | bytes 10485760 | tf_op jit(solution)/shard_map/all_gather | solution.py:59
  56.0 54.6 %all-to-all-start = ((bf16[8,2,65536]{2,1,0:T(2,128)(2,1)}), bf16[8,2,65536]{2,1,0:T(2,128)(2,1)S(1)}, u32[]{:S(2)}, u32[]{:S(2)}) async-start(bf16[8,2,65536]{2,1,0:T(2,128)(2,1)} %reshape.226), calls=%async_computation | async-start | bytes 4194304 | tf_op jit(solution)/shard_map/all_to_all | solution.py:66
  94.7 20.5 %copy-start.3 = (s32[4,2]{0,1:T(2,128)S(1)}, s32[4,2]{0,1:T(2,128)}, u32[]{:S(2)}) copy-start(s32[4,2]{0,1:T(2,128)} %param.8) | copy-start | bytes 100
  110.5 52.3 %all-to-all-start.2 = ((bf16[8,2,65536]{2,1,0:T(2,128)(2,1)}), bf16[8,2,65536]{2,1,0:T(2,128)(2,1)}, u32[]{:S(2)}, u32[]{:S(2)}) async-start(bf16[8,2,65536]{2,1,0:T(2,128)(2,1)} %reshape.224), calls=%async_computation.2 | async-start | bytes 4194304 | tf_op jit(solution)/shard_map/all_to_all | solution.py:67
  114.9 272.5 %reduce-scatter.2.cloned.1.call-start = ((), (), s32[]{:S(2)}) async-start(), calls=%async_computation.7 | async-start | bytes 10485760 | tf_op jit(solution)/shard_map/reduce_scatter | solution.py:76
  185.4 4.5 %copy-start.2 = (bf16[1,256,4,1,128]{4,3,2,1,0:T(2,128)(2,1)S(1)}, bf16[1,256,4,1,128]{4,3,2,1,0:T(2,128)(2,1)}, u32[]{:S(2)}) copy-start(bf16[1,256,4,1,128]{4,3,2,1,0:T(2,128)(2,1)} %get-tuple-element.40) | copy-start | bytes 786436
  202.5 15.9 %copy-start = (bf16[1,2,128,2048]{3,2,1,0:T(8,128)(2,1)S(1)}, bf16[1,2,128,2048]{3,2,1,0:T(8,128)(2,1)}, u32[]{:S(2)}) copy-start(bf16[1,2,128,2048]{3,2,1,0:T(8,128)(2,1)} %all-gather.3.cloned.1.call-done) | copy-start | bytes 3145732
  267.6 51.5 %all-to-all-start.3 = ((bf16[8,2,65536]{2,1,0:T(2,128)(2,1)}), bf16[8,2,65536]{2,1,0:T(2,128)(2,1)S(1)}, u32[]{:S(2)}, u32[]{:S(2)}) async-start(bf16[8,2,65536]{2,1,0:T(2,128)(2,1)} %reshape.230), calls=%async_computation.3 | async-start | bytes 4194304 | tf_op jit(solution)/shard_map/all_to_all | solution.py:72
  319.1 52.4 %all-to-all-start.1 = ((bf16[8,2,65536]{2,1,0:T(2,128)(2,1)}), bf16[8,2,65536]{2,1,0:T(2,128)(2,1)}, u32[]{:S(2)}, u32[]{:S(2)}) async-start(bf16[8,2,65536]{2,1,0:T(2,128)(2,1)} %reshape.228), calls=%async_computation.1 | async-start | bytes 4194304 | tf_op jit(solution)/shard_map/all_to_all | solution.py:71
Sparse Core Ops, SparseCore 0:
  20.3 40.1 all-gather.2
  62.6 57.2 all-gather.4
  224.2 69.8 reduce-scatter.1
where the time goes:
time: 409 us; the launch traced here: 401 us
  local copies, waits for them, and re-layouts  125 us (31%)
  waiting for transfers between devices  91 us (22%)
  other arithmetic  74.5 us (18%)
  matrix products  66.5 us (16%)
  starting transfers between devices  18.8 us (5%)
  between operations  16.1 us (4%)
  blocking collectives  8.89 us (2%)
    unnamed x28, local copies, waits for them, and re-layouts  88.7 us
    unnamed x4, other arithmetic  73.6 us
    all_to_all x1, waiting for transfers between devices, per_device(): lax.all_to_all(grad_out, 'ctx', split_axis=2, concat_axis=1, tiled=True)  36.9 us
    all_to_all x1, waiting for transfers between devices, per_device(): lax.all_to_all(head_out, 'ctx', split_axis=1, concat_axis=2, tiled=True)  34.2 us
    dot_general x1, matrix products, attend(): jnp.einsum('bhlj,bjhd->blhd', grad_scores, key, preferred_element_type=jn...  18.2 us
    dot_general x1, matrix products, attend(): jnp.einsum('bhlj,blhd->bjhd', grad_scores, q_rows, preferred_element_type...  14.9 us
    convert_element_type x1, local copies, waits for them, and re-layouts, attend(): attended = attended.reshape(batch, length, width).astype(jnp.bfloat16)  10.8 us
    all_to_all x1, waiting for transfers between devices, per_device(): lax.all_to_all(queries, 'ctx', split_axis=2, concat_axis=1, tiled=True)  9.97 us
  transfers between devices with their start and end apart: 7, of which 4 were waited for; matrix products, arithmetic and copies ran while one was open for 53% of the time, Pallas kernels for 0%

commit v1 on v0

--- a/solution.py
+++ b/solution.py
@@ -64,7 +64,15 @@
     valid = (positions[None, None, :] < chosen_lengths[:, :, None]).reshape(per_group, 2 * tokens)
     moved_queries, moved_grads = (
         lax.all_to_all(queries, "ctx", split_axis=2, concat_axis=1, tiled=True),
-        lax.all_to_all(grad_out, "ctx", split_axis=2, concat_axis=1, tiled=True),
+        jnp.concatenate(
+            jax.lax.all_to_all(
+                jnp.stack(jnp.split(grad_out, jax.lax.axis_size("ctx"), axis=2), axis=0),
+                "ctx",
+                0,
+                0,
+            ),
+            axis=1,
+        ),
     )
     head_out, head_grad, grad_kv = attend(moved_queries, kv_local, valid, moved_grads)
     attended, grad_queries = (

time: 409 us -> 387 us (0.946); the launches traced: 401 us -> 385 us
  other arithmetic: 74.5 us -> 51.7 us
  waiting for transfers between devices: 91 us -> 109 us
  local copies, waits for them, and re-layouts: 125 us -> 116 us
    all_to_all x1, waiting for transfers between devices: 9.97 us -> 39.7 us  [per_device(): lax.all_to_all(queries, 'ctx', split_axis=2, concat_axis=1, tiled=True)]
    unnamed x4 -> x3, other arithmetic: 73.6 us -> 50.8 us
    unnamed x28 -> x33, local copies, waits for them, and re-layouts: 88.7 us -> 75 us
    all_to_all x1, waiting for transfers between devices: 36.9 us -> 25 us  [per_device(): jax.lax.all_to_all(jnp.stack(jnp.split(grad_out, jax.lax.axis_size('ctx')...]
    another operation x2 -> x4, local copies, waits for them, and re-layouts: 5.22 us -> 12.4 us
  transfers between devices with their start and end apart: 7 -> 7, of which waited for: 4 -> 4; matrix products, arithmetic and copies ran while one was open for 53% -> 47% of each run, Pallas kernels for 0% -> 0%
where the time goes in v1:
time: 387 us; the launch traced here: 385 us
  local copies, waits for them, and re-layouts  116 us (30%)
  waiting for transfers between devices  109 us (28%)
  matrix products  66.5 us (17%)
  other arithmetic  51.7 us (13%)
  starting transfers between devices  17.8 us (5%)
  between operations  15.9 us (4%)
  blocking collectives  8.89 us (2%)
    unnamed x33, local copies, waits for them, and re-layouts  75 us
    unnamed x3, other arithmetic  50.8 us
    all_to_all x1, waiting for transfers between devices, per_device(): lax.all_to_all(queries, 'ctx', split_axis=2, concat_axis=1, tiled=True)  39.7 us
    all_to_all x1, waiting for transfers between devices, per_device(): lax.all_to_all(head_out, 'ctx', split_axis=1, concat_axis=2, tiled=True)  34.1 us
    all_to_all x1, waiting for transfers between devices, per_device(): jax.lax.all_to_all(jnp.stack(jnp.split(grad_out, jax.lax.axis_size('ctx')...  25 us
    dot_general x1, matrix products, attend(): jnp.einsum('bhlj,bjhd->blhd', grad_scores, key, preferred_element_type=jn...  18.2 us
    dot_general x1, matrix products, attend(): jnp.einsum('bhlj,blhd->bjhd', grad_scores, q_rows, preferred_element_type...  14.9 us
    convert_element_type x1, local copies, waits for them, and re-layouts, attend(): attended = attended.reshape(batch, length, width).astype(jnp.bfloat16)  10.8 us
  transfers between devices with their start and end apart: 7, of which 4 were waited for; matrix products, arithmetic and copies ran while one was open for 47% of the time, Pallas kernels for 0%

profile of v1, /device:TPU:0, one launch (start us, length us, event | category | flops | bytes accessed | tf_op | source)
XLA Modules:
  0.0 385.1 jit_solution(16305777681979383123)
XLA Ops:
  7.2 0.0 all-gather.3.cloned.1.call-start
  7.2 1.2 dynamic_slice.3
  10.4 8.9 %all_gather.9 = bf16[4,2,128,256]{3,2,1,0:T(8,128)(2,1)S(1)} all-gather(bf16[1,2,128,256]{3,2,1,0:T(8,128)(2,1)} %param.6), channel_id=1, replica_groups=mesh['dp'=4,'ctx'=8] {'dp'}, dimensions={0}, use_global_device_ids=true | all-gather | bytes 655360 | tf_op jit(solution)/shard_map/all_gather | solution.py:50
  19.3 0.7 dynamic-slice_select_fusion
  20.0 0.0 all-gather.5.cloned.1.call-start
  20.0 3.5 copy.83
  23.6 1.8 bitcast_dynamic-update-slice_fusion.7
  25.4 1.7 bitcast_dynamic-update-slice_fusion.6
  27.1 1.7 bitcast_dynamic-update-slice_fusion.5
  28.8 1.7 bitcast_dynamic-update-slice_fusion.4
  30.5 1.7 bitcast_dynamic-update-slice_fusion.3
  32.1 1.7 bitcast_dynamic-update-slice_fusion.2
  33.8 1.7 bitcast_dynamic-update-slice_fusion.1
  35.5 1.7 bitcast_dynamic-update-slice_fusion
  37.2 5.8 %all-to-all-start.2 = ((bf16[8,1,256,512]{3,2,1,0:T(8,128)(2,1)}), bf16[8,1,256,512]{3,2,1,0:T(8,128)(2,1)}, u32[]{:S(2)}, u32[]{:S(2)}) async-start(bf16[8,1,256,512]{3,2,1,0:T(8,128)(2,1)} %bitcast_dynamic-update-slice_fusion), calls=%async_computation.2 | async-start | bytes 4194304 | tf_op jit(solution)/shard_map/all_to_all | solution.py:68
  43.0 7.1 %copy.86 = bf16[1,256,4096]{1,0,2:T(2,128)(2,1)} copy(bf16[1,256,4096]{2,1,0:T(8,128)(2,1)S(1)} %copy-done.2) | data formatting | bytes 4194304 | tf_op args[4]
  50.0 0.5 broadcast.122
  50.5 21.5 %reduce.8 = bf16[4096,256]{1,0:T(8,128)(2,1)S(1)} reduce(bf16[4096,1,256]{2,1,0:T(2,128)(2,1)} %bitcast.117, bf16[]{:T(256)} %broadcast.122), dimensions={1}, to_apply=%bitcast.98.reduce_sub_computation | reduce | bytes 4194306
  72.0 3.2 reshape.223
  75.2 25.0 %all-to-all-done.2 = bf16[8,1,256,512]{3,2,1,0:T(8,128)(2,1)} async-done(((bf16[8,1,256,512]{3,2,1,0:T(8,128)(2,1)}), bf16[8,1,256,512]{3,2,1,0:T(8,128)(2,1)}, u32[]{:S(2)}, u32[]{:S(2)}) %all-to-all-start.2) | async-done | bytes 2097184 | tf_op jit(solution)/shard_map/all_to_all | solution.py:68
  100.2 3.6 all-to-all-start
  103.9 0.0 reduce-scatter.2.cloned.1.call-start
  103.9 0.2 fusion.44
  104.1 0.1 lt.36
  104.2 4.0 %reshape.221 = bf16[2048,4,128]{2,1,0:T(4,128)(2,1)} reshape(bf16[8,1,256,512]{3,2,1,0:T(8,128)(2,1)} %all-to-all-done.2) | data formatting | bytes 4194304 | tf_op jit(solution)/shard_map/reshape.25
  108.1 4.4 %copy.109 = bf16[2048,4,128]{0,2,1:T(8,128)(2,1)} copy(bf16[2048,4,128]{2,1,0:T(4,128)(2,1)} %reshape.221) | data formatting | bytes 4194304 | tf_op jit(solution)/shard_map/reshape.25
  112.5 39.7 %all-to-all-done = bf16[8,2,65536]{2,1,0:T(2,128)(2,1)S(1)} async-done(((bf16[8,2,65536]{2,1,0:T(2,128)(2,1)}), bf16[8,2,65536]{2,1,0:T(2,128)(2,1)S(1)}, u32[]{:S(2)}, u32[]{:S(2)}) %all-to-all-start) | async-done | bytes 2097184 | tf_op jit(solution)/shard_map/all_to_all | solution.py:66
  152.3 4.3 %reshape.224 = bf16[4096,1,256]{2,1,0:T(2,128)(2,1)} reshape(bf16[8,2,65536]{2,1,0:T(2,128)(2,1)S(1)} %all-to-all-done) | data formatting | bytes 4194304
  156.6 2.5 copy.120
  159.1 1.2 copy.87
  160.3 2.3 reshape.170
  162.7 5.0 %fusion.24 = bf16[1,2,128,1024]{3,2,1,0:T(8,128)(2,1)S(1)} fusion(bf16[2048,2,1024]{2,0,1:T(8,128)(2,1)} %all-gather.5.cloned.1.call-done, bf16[1,2,128,2048]{3,2,1,0:T(8,128)(2,1)} %all-gather.3.cloned.1.call-done), kind=kOutput, calls=%fused_computation.23 | convolution fusion | flops 1074003968 | bytes 9961472 | tf_op jit(solution)/shard_map/betf,fec->betc/dot_general | solution.py:56
  167.6 0.4 reshape.167
  168.0 1.5 fusion.51
  169.5 0.6 copy.123
  170.2 4.5 %fusion.41 = f32[4,2048,256]{1,2,0:T(8,128)} fusion(bf16[2048,4,128]{0,2,1:T(8,128)(2,1)S(1)} %copy-done.1, bf16[1,256,4,1,128]{1,4,2,3,0:T(8,128)(2,1)S(1)} %copy.123), kind=kOutput, calls=%fused_computation.41 | convolution fusion | flops 536870912 | bytes 10747904 | tf_op jit(solution)/shard_map/blhd,bjhd->bhlj/dot_general | solution.py:28
  174.7 8.0 %fusion.52 = (f32[4,2048]{1,0:T(4,128)S(1)}, f32[4,2048,256]{1,2,0:T(8,128)}) fusion(pred[256]{0:T(512)(128)(4,1)S(1)} %bitcast_compare_fusion, bf16[2048,4,128]{0,2,1:T(8,128)(2,1)} %reshape.170, bf16[1,256,4,1,128]{4,3,2,1,0:T(2,128)(2,1)S(1)} %copy-done.3), kind=kOutput, calls=%fused_computation.55 | convolution fusion | flops 545259776 | bytes 10780928 | tf_op jit(solution)/shard_map/sub | solution.py:23
  182.7 4.6 %fusion.31 = bf16[1,256,4,1,128]{4,1,2,3,0:T(8,128)(2,1)S(1)} fusion(bf16[2048,4,128]{0,2,1:T(8,128)(2,1)S(1)} %copy-done.1, f32[4,2048,256]{1,2,0:T(8,128)} %get-tuple-element.43, f32[4,2048]{1,0:T(4,128)S(1)} %get-tuple-element.42), kind=kOutput, calls=%fused_computation.26 | convolution fusion | flops 541196288 | bytes 10780672 | tf_op jit(solution)/shard_map/bhlj,blhd->bjhd/dot_general | solution.py:38
  187.4 14.9 %fusion.34 = bf16[1,256,4,1,128]{4,1,2,3,0:T(8,128)(2,1)S(1)} fusion(bf16[2048,4,128]{0,2,1:T(8,128)(2,1)} %reshape.170, f32[4,2048,256]{1,2,0:T(8,128)} %fusion.41, f32[4,2048,256]{1,2,0:T(8,128)} %get-tuple-element.43, f32[4,2048]{1,0:T(4,128)S(1)} %get-tuple-element.42), kind=kOutput, calls=%fused_computation.27 | convolution fusion | flops 551690496 | bytes 19169280 | tf_op jit(solution)/shard_map/bhlj,blhd->bjhd/dot_general | solution.py:35
  202.3 0.1 pad_maximum_fusion
  202.3 0.5 copy.102
  202.9 0.4 convert_element_type.90
  203.2 5.6 %convert_bitcast_fusion = bf16[2048,2,1024]{0,2,1:T(8,128)(2,1)} fusion(bf16[2,128,1024]{2,1,0:T(8,128)(2,1)S(1)} %convert_element_type.90, bf16[1,2,128,2048]{3,2,1,0:T(8,128)(2,1)S(1)} %copy-done), kind=kOutput, calls=%fused_computation.6 | convolution fusion | flops 1077936128 | bytes 9961472 | tf_op jit(solution)/shard_map/betf,betc->fec/dot_general | solution.py:85
  208.9 18.2 %fusion.18 = bf16[4,128,2048]{2,1,0:T(8,128)(2,1)S(1)} fusion(f32[4,2048,256]{1,2,0:T(8,128)} %fusion.41, bf16[1,256,4,1,128]{4,3,2,1,0:T(2,128)(2,1)S(1)} %copy-done.3, f32[4,2048,256]{1,2,0:T(8,128)} %get-tuple-element.43, f32[4,2048]{1,0:T(4,128)S(1)} %get-tuple-element.42), kind=kOutput, calls=%fused_computation.17 | convolution fusion | flops 552608000 | bytes 19169280 | tf_op jit(solution)/shard_map/bhlj,bjhd->blhd/dot_general | solution.py:31
  227.1 7.5 %copy.97 = bf16[1,2048,512]{2,0,1:T(2,128)(2,1)} copy(bf16[1,2048,512]{1,2,0:T(8,128)(2,1)S(1)} %bitcast.129) | data formatting | bytes 4194304 | tf_op jit(solution)/shard_map/convert_element_type | solution.py:34
  234.6 14.0 %reduce.10 = bf16[2048,512]{1,0:T(8,128)(2,1)S(1)} reduce(bf16[2048,1,512]{2,1,0:T(2,128)(2,1)} %bitcast.120, bf16[]{:T(256)} %broadcast.122), dimensions={1}, to_apply=%bitcast.102.reduce_sub_computation | reduce | bytes 4194306
  248.6 3.8 reshape.227
  252.4 3.6 all-to-all-start.3
  256.0 5.7 %convolution_convert_fusion = bf16[4,128,2048]{2,1,0:T(8,128)(2,1)} fusion(bf16[1,256,4,1,128]{1,4,2,3,0:T(8,128)(2,1)S(1)} %copy.123, f32[4,2048,256]{1,2,0:T(8,128)} %get-tuple-element.43, f32[4,2048]{1,0:T(4,128)S(1)} %get-tuple-element.42), kind=kOutput, calls=%fused_computation.18 | convolution fusion | flops 542113792 | bytes 10780672 | tf_op jit(solution)/shard_map/bhlj,bjhd->blhd/dot_general | solution.py:26
  261.7 10.8 %copy.90 = bf16[1,2048,512]{2,0,1:T(2,128)(2,1)} copy(bf16[1,2048,512]{1,2,0:T(8,128)(2,1)} %bitcast.128) | data formatting | bytes 4194304 | tf_op jit(solution)/shard_map/convert_element_type | solution.py:27
  272.5 15.3 %reduce.9 = bf16[2048,512]{1,0:T(8,128)(2,1)} reduce(bf16[2048,1,512]{2,1,0:T(2,128)(2,1)} %bitcast.118, bf16[]{:T(256)} %broadcast.122), dimensions={1}, to_apply=%bitcast.100.reduce_sub_computation | reduce | bytes 4194306
  287.8 6.3 %reshape.225 = bf16[8,2,65536]{2,1,0:T(2,128)(2,1)} reshape(bf16[2048,512]{1,0:T(8,128)(2,1)} %reduce.9) | data formatting | bytes 4194304
  294.1 9.8 %all-to-all-done.3 = bf16[8,2,65536]{2,1,0:T(2,128)(2,1)S(1)} async-done(((bf16[8,2,65536]{2,1,0:T(2,128)(2,1)}), bf16[8,2,65536]{2,1,0:T(2,128)(2,1)S(1)}, u32[]{:S(2)}, u32[]{:S(2)}) %all-to-all-start.3) | async-done | bytes 2097184 | tf_op jit(solution)/shard_map/all_to_all | solution.py:80
  303.8 4.6 %all-to-all-start.1 = ((bf16[8,2,65536]{2,1,0:T(2,128)(2,1)}), bf16[8,2,65536]{2,1,0:T(2,128)(2,1)}, u32[]{:S(2)}, u32[]{:S(2)}) async-start(bf16[8,2,65536]{2,1,0:T(2,128)(2,1)} %reshape.225), calls=%async_computation.1 | async-start | bytes 4194304 | tf_op jit(solution)/shard_map/all_to_all | solution.py:79
  308.5 4.3 %reshape.228 = bf16[2048,1,512]{2,1,0:T(2,128)(2,1)} reshape(bf16[8,2,65536]{2,1,0:T(2,128)(2,1)S(1)} %all-to-all-done.3) | data formatting | bytes 4194304
  312.8 2.8 copy.122
  315.6 2.4 copy.98
  318.0 4.1 %copy.105 = bf16[1,256,4096]{2,1,0:T(8,128)(2,1)} copy(bf16[1,256,4096]{1,2,0:T(8,128)(2,1)} %bitcast.126) | data formatting | bytes 4194304
  322.0 34.1 %all-to-all-done.1 = bf16[8,2,65536]{2,1,0:T(2,128)(2,1)} async-done(((bf16[8,2,65536]{2,1,0:T(2,128)(2,1)}), bf16[8,2,65536]{2,1,0:T(2,128)(2,1)}, u32[]{:S(2)}, u32[]{:S(2)}) %all-to-all-start.1) | async-done | bytes 2097184 | tf_op jit(solution)/shard_map/all_to_all | solution.py:79
  356.1 6.7 %reshape.226 = bf16[2048,1,512]{2,1,0:T(2,128)(2,1)} reshape(bf16[8,2,65536]{2,1,0:T(2,128)(2,1)} %all-to-all-done.1) | data formatting | bytes 4194304
  362.9 2.8 copy.121
  365.7 2.4 copy.91
  368.0 4.1 %copy.104 = bf16[1,256,4096]{2,1,0:T(8,128)(2,1)} copy(bf16[1,256,4096]{1,2,0:T(8,128)(2,1)} %bitcast.127) | data formatting | bytes 4194304
  372.1 6.5 %copy.106 = f32[512,2,1024]{2,1,0:T(2,128)} copy(bf16[512,2,1024]{0,2,1:T(8,128)(2,1)} %reduce-scatter.2.cloned.1.call-done) | data formatting | bytes 6291456
  (17 shorter events, 0.1 us)
Async XLA Ops:
  7.2 155.5 %all-gather.3.cloned.1.call-start = ((), (), s32[]{:S(2)}) async-start(), calls=%async_computation.5 | async-start | bytes 1179648 | tf_op jit(solution)/shard_map/all_gather | solution.py:53
  20.0 142.7 %all-gather.5.cloned.1.call-start = ((), (), s32[]{:S(2)}) async-start(), calls=%async_computation.6 | async-start | bytes 10485760 | tf_op jit(solution)/shard_map/all_gather | solution.py:59
  23.6 19.4 %copy-start.2 = (bf16[1,256,4096]{2,1,0:T(8,128)(2,1)S(1)}, bf16[1,256,4096]{2,1,0:T(8,128)(2,1)}, u32[]{:S(2)}) copy-start(bf16[1,256,4096]{2,1,0:T(8,128)(2,1)} %param.10) | copy-start | bytes 6291460
  37.2 63.1 %all-to-all-start.2 = ((bf16[8,1,256,512]{3,2,1,0:T(8,128)(2,1)}), bf16[8,1,256,512]{3,2,1,0:T(8,128)(2,1)}, u32[]{:S(2)}, u32[]{:S(2)}) async-start(bf16[8,1,256,512]{3,2,1,0:T(8,128)(2,1)} %bitcast_dynamic-update-slice_fusion), calls=%async_computation.2 | async-start | bytes 4194304 | tf_op jit(solution)/shard_map/all_to_all | solution.py:68
  72.0 31.9 %copy-start.4 = (s32[4,2]{0,1:T(2,128)S(1)}, s32[4,2]{0,1:T(2,128)}, u32[]{:S(2)}) copy-start(s32[4,2]{0,1:T(2,128)} %param.8) | copy-start | bytes 100
  100.2 52.0 %all-to-all-start = ((bf16[8,2,65536]{2,1,0:T(2,128)(2,1)}), bf16[8,2,65536]{2,1,0:T(2,128)(2,1)S(1)}, u32[]{:S(2)}, u32[]{:S(2)}) async-start(bf16[8,2,65536]{2,1,0:T(2,128)(2,1)} %reshape.223), calls=%async_computation | async-start | bytes 4194304 | tf_op jit(solution)/shard_map/all_to_all | solution.py:66
  103.9 268.3 %reduce-scatter.2.cloned.1.call-start = ((), (), s32[]{:S(2)}) async-start(), calls=%async_computation.7 | async-start | bytes 10485760 | tf_op jit(solution)/shard_map/reduce_scatter | solution.py:84
  167.6 2.6 copy-start.1
  170.2 4.5 %copy-start.3 = (bf16[1,256,4,1,128]{4,3,2,1,0:T(2,128)(2,1)S(1)}, bf16[1,256,4,1,128]{4,3,2,1,0:T(2,128)(2,1)}, u32[]{:S(2)}) copy-start(bf16[1,256,4,1,128]{4,3,2,1,0:T(2,128)(2,1)} %get-tuple-element.40) | copy-start | bytes 786436
  187.4 15.9 %copy-start = (bf16[1,2,128,2048]{3,2,1,0:T(8,128)(2,1)S(1)}, bf16[1,2,128,2048]{3,2,1,0:T(8,128)(2,1)}, u32[]{:S(2)}) copy-start(bf16[1,2,128,2048]{3,2,1,0:T(8,128)(2,1)} %all-gather.3.cloned.1.call-done) | copy-start | bytes 3145732
  252.4 51.4 %all-to-all-start.3 = ((bf16[8,2,65536]{2,1,0:T(2,128)(2,1)}), bf16[8,2,65536]{2,1,0:T(2,128)(2,1)S(1)}, u32[]{:S(2)}, u32[]{:S(2)}) async-start(bf16[8,2,65536]{2,1,0:T(2,128)(2,1)} %reshape.227), calls=%async_computation.3 | async-start | bytes 4194304 | tf_op jit(solution)/shard_map/all_to_all | solution.py:80
  303.8 52.3 %all-to-all-start.1 = ((bf16[8,2,65536]{2,1,0:T(2,128)(2,1)}), bf16[8,2,65536]{2,1,0:T(2,128)(2,1)}, u32[]{:S(2)}, u32[]{:S(2)}) async-start(bf16[8,2,65536]{2,1,0:T(2,128)(2,1)} %reshape.225), calls=%async_computation.1 | async-start | bytes 4194304 | tf_op jit(solution)/shard_map/all_to_all | solution.py:79
Sparse Core Ops, SparseCore 0:
  20.1 51.1 all-gather.2
  73.4 65.7 all-gather.4
  209.0 69.8 reduce-scatter.1
